TPU v7x, 32 devices: a whole 2x2x4 slice. The times are simulated.
32 devices in a mesh: groups: 2 (over y), cols: 4 (over z), rows: 4 (over x, core).
Axes of the slice: x: 2, y: 2, z: 4, core: 2. Of those that a mesh axis runs over, the one named last changes fastest.
Arguments:
- base_field: float32 [320, 64, 512], P(None, ('groups', 'cols'), 'rows'), parts along dimension 1, may hold values from -6 to 6
- control_field: float32 [320, 64, 512], P(None, ('groups', 'cols', 'rows')), parts along dimension 1, may hold values from -6 to 6
- first_kernel: bfloat16 [9, 320, 320], replicated, may hold values from -0.109375 to 0.109375
- second_kernel: bfloat16 [9, 320, 320], replicated, may hold values from -0.109375 to 0.109375
- control_kernel: bfloat16 [9, 320, 320], replicated, may hold values from -0.109375 to 0.109375
- first_bias: float32 [320], replicated, may hold values from -3 to 3
- second_bias: float32 [320], replicated, may hold values from -3 to 3
- control_bias: float32 [320], replicated, may hold values from -3 to 3
- to_control: bfloat16 [320, 320], replicated, may hold values from -0.3125 to 0.3125
- to_base: bfloat16 [320, 320], replicated, may hold values from -0.3125 to 0.3125
Outputs:
- base_out: float32 [320, 64, 512], P(None, ('groups', 'cols'), 'rows'), parts along dimension 1
- control_out: float32 [320, 64, 512], P(None, ('groups', 'cols', 'rows')), parts along dimension 1
There are 2 independent parts, one for each index of `groups`. A program takes and returns all parts, laid end to end along the dimension named above; an argument that names none is the same for every part. Nothing has to cross between parts.
All inputs are finite; a program needn't handle non-finite values.
Results may differ from a plain program's by a relative error of at most 0.0033.
Values may be sent and summed in bfloat16 or wider, within the bound.
A program may use at most 64 MiB of HBM per device.

v0:
```python
import jax
import jax.numpy as jnp
from jax import lax
from jax.sharding import PartitionSpec as P


def padded_2(value, sides, width):
    for axis, dim in sides:
        count, length = (lax.axis_size(axis), value.shape[dim])
        up = [(i, (i + 1) % count) for i in range(count - 1)]
        down = [(j, i) for i, j in up]
        last = lax.slice_in_dim(value, length - width, length, axis=dim)
        leading = lax.slice_in_dim(value, 0, width, axis=dim)
        before = lax.ppermute(last, axis, up)
        after = lax.ppermute(leading, axis, down)
        value = jnp.concatenate([before, value, after], axis=dim)
    return value


def convolve(padded, weight, bias):
    width = padded.shape[1] - 2
    height = padded.shape[2] - 2
    total = jnp.zeros((weight.shape[1], width, height), jnp.float32)
    for offset in range(9):
        across = offset // 3
        down = offset % 3
        window = padded[:, across : across + width, down : down + height]
        total = total + jnp.einsum(
            "oc,cwh->owh", weight[offset], window, preferred_element_type=jnp.float32
        )
    return total + bias[:, None, None]


def project(matrix, field):
    return jnp.einsum("oc,cwh->owh", matrix, field, preferred_element_type=jnp.float32)


def per_device(
    base_field,
    control_field,
    first_kernel,
    second_kernel,
    control_kernel,
    first_bias,
    second_bias,
    control_bias,
    to_control,
    to_base,
):
    base_round = base_field.astype(jnp.bfloat16)
    tile_cols = base_field.shape[1]
    tile_rows = base_field.shape[2]
    padded = padded_2(base_round, (("cols", 1), ("rows", 2)), 2)
    inner = jax.nn.silu(convolve(padded, first_kernel, first_bias))
    across = lax.axis_index("cols") * tile_cols - 1 + jnp.arange(tile_cols + 2, dtype=jnp.int32)
    downward = lax.axis_index("rows") * tile_rows - 1 + jnp.arange(tile_rows + 2, dtype=jnp.int32)
    col_inside = (across >= 0) & (across < tile_cols * lax.axis_size("cols"))
    row_inside = (downward >= 0) & (downward < tile_rows * lax.axis_size("rows"))
    inside = col_inside[:, None] & row_inside[None, :]
    hidden_ext = jnp.where(inside[None], inner, 0.0).astype(jnp.bfloat16)
    base_mid = jax.nn.silu(convolve(hidden_ext, second_kernel, second_bias)) + base_field
    base_send = base_mid.astype(jnp.bfloat16)
    control_round = control_field.astype(jnp.bfloat16)
    edged = padded_2(control_round, ((("cols", "rows"), 1),), 1)
    edged = jnp.pad(edged, ((0, 0), (0, 0), (1, 1)))
    control_mid = jax.nn.silu(convolve(edged, control_kernel, control_bias)) + control_field
    arrived = lax.all_to_all(base_send, "rows", split_axis=1, concat_axis=2, tiled=True)
    control_out = control_mid + project(to_control, arrived)
    control_send = control_out.astype(jnp.bfloat16)
    returned = lax.all_to_all(control_send, "rows", split_axis=2, concat_axis=1, tiled=True)
    base_out = base_mid + project(to_base, returned)
    return (base_out, control_out)


def solution(mesh):
    return jax.shard_map(
        per_device,
        mesh=mesh,
        in_specs=(
            P(None, ("groups", "cols"), "rows"),
            P(None, ("groups", "cols", "rows"), None),
            P(),
            P(),
            P(),
            P(),
            P(),
            P(),
            P(),
            P(),
        ),
        out_specs=(P(None, ("groups", "cols"), "rows"), P(None, ("groups", "cols", "rows"), None)),
        check_vma=False,
    )
```

profile of v0, /device:TPU:0, one launch (start us, length us, event | category | flops | bytes accessed | tf_op | source)
XLA Modules:
  0.0 80.0 jit_solution(4251604718525200333)
XLA Ops:
  0.7 1.8 %copy.29 = bf16[320,8,128]{0,2,1:T(8,128)(2,1)S(1)} copy(f32[320,8,128]{2,1,0:T(8,128)} %param.10) | data formatting | bytes 1966080 | tf_op args[0]
  2.5 0.8 fusion.120
  3.3 1.3 %collective-permute-start.1 = (bf16[320,2,128]{0,2,1:T(8,128)(2,1)}, bf16[320,2,128]{0,2,1:T(8,128)(2,1)S(1)}, u32[]{:S(2)}, u32[]{:S(2)}) collective-permute-start(bf16[320,2,128]{0,2,1:T(8,128)(2,1)} %get-tuple-element.9), channel_id=1, source_target_pairs={{4,0},{8,4},{12,8},{5,1},{9,5},{13,9},{6,2},{10,6},{14,10},{7,3},{... | collective-permute-start | bytes 491528 | tf_op jit(solution)/shard_map/ppermute | solution.py:15
  4.5 5.6 %collective-permute-start = (bf16[320,2,128]{0,2,1:T(8,128)(2,1)}, bf16[320,2,128]{0,2,1:T(8,128)(2,1)S(1)}, u32[]{:S(2)}, u32[]{:S(2)}) collective-permute-start(bf16[320,2,128]{0,2,1:T(8,128)(2,1)} %get-tuple-element.8), channel_id=1, source_target_pairs={{0,4},{4,8},{8,12},{1,5},{5,9},{9,13},{2,6},{6,10},{10,14},{3,7},{... | collective-permute-start | bytes 491528 | tf_op jit(solution)/shard_map/ppermute | solution.py:14
  10.4 0.9 %fusion.121 = (bf16[320,1,512]{2,0,1:T(8,128)(2,1)}, bf16[320,1,512]{2,0,1:T(8,128)(2,1)}) fusion(bf16[320,2,512]{2,0,1:T(8,128)(2,1)S(1)} %copy.64), kind=kLoop, calls=%fused_computation.151 | loop fusion | bytes 1310720 | tf_op jit(solution)/shard_map/slice | solution.py:12
  11.2 1.3 %collective-permute-start.5 = (bf16[320,1,512]{2,0,1:T(8,128)(2,1)}, bf16[320,1,512]{2,0,1:T(8,128)(2,1)}, u32[]{:S(2)}, u32[]{:S(2)}) collective-permute-start(bf16[320,1,512]{2,0,1:T(8,128)(2,1)} %get-tuple-element.11), channel_id=1, source_target_pairs={{1,0},{2,1},{3,2},{4,3},{5,4},{6,5},{7,6},{8,7},{9,8},{10,9},{11,1... | collective-permute-start | bytes 983048 | tf_op jit(solution)/shard_map/ppermute | solution.py:15
  12.5 3.8 %collective-permute-start.4 = (bf16[320,1,512]{2,0,1:T(8,128)(2,1)}, bf16[320,1,512]{2,0,1:T(8,128)(2,1)}, u32[]{:S(2)}, u32[]{:S(2)}) collective-permute-start(bf16[320,1,512]{2,0,1:T(8,128)(2,1)} %get-tuple-element.10), channel_id=1, source_target_pairs={{0,1},{1,2},{2,3},{3,4},{4,5},{5,6},{6,7},{7,8},{8,9},{9,10},{10,1... | collective-permute-start | bytes 983048 | tf_op jit(solution)/shard_map/ppermute | solution.py:14
  16.3 1.4 %fusion.59 = f32[320,2,512]{2,0,1:T(8,128)S(1)} fusion(bf16[320,2,512]{2,0,1:T(8,128)(2,1)S(1)} %copy.64, bf16[9,320,320]{2,1,0:T(8,128)(2,1)} %param.14), kind=kOutput, calls=%fused_computation.85 | convolution fusion | flops 209715200 | bytes 2211840 | tf_op jit(solution)/shard_map/oc,cwh->owh/dot_general | solution.py:28
  17.8 1.4 %collective-permute-start.3 = (bf16[320,12,2]{0,2,1:T(2,128)(2,1)S(1)}, bf16[320,12,2]{0,2,1:T(2,128)(2,1)S(1)}, u32[]{:S(2)}, u32[]{:S(2)}) collective-permute-start(bf16[320,12,2]{0,2,1:T(2,128)(2,1)S(1)} %get-tuple-element.7), channel_id=1, source_target_pairs={{1,0},{2,1},{3,2},{5,4},{6,5},{7,6},{9,8},{10,9},{11,10},{13,12},{... | collective-permute-start | bytes 46088 | tf_op jit(solution)/shard_map/ppermute | solution.py:15
  19.3 3.4 %collective-permute-start.2 = (bf16[320,12,2]{0,2,1:T(2,128)(2,1)S(1)}, bf16[320,12,2]{0,2,1:T(2,128)(2,1)S(1)}, u32[]{:S(2)}, u32[]{:S(2)}) collective-permute-start(bf16[320,12,2]{0,2,1:T(2,128)(2,1)S(1)} %get-tuple-element.6), channel_id=1, source_target_pairs={{0,1},{1,2},{2,3},{4,5},{5,6},{6,7},{8,9},{9,10},{10,11},{12,13},{... | collective-permute-start | bytes 46088 | tf_op jit(solution)/shard_map/ppermute | solution.py:14
  24.0 0.8 %fusion.24 = f32[10,130,320]{2,1,0:T(8,128)S(1)} fusion(bf16[320,12,132]{0,2,1:T(8,128)(2,1)S(1)} %pad_maximum_fusion, bf16[9,320,320]{2,1,0:T(8,128)(2,1)S(1)} %copy-done.5), kind=kOutput, calls=%fused_computation.48 | convolution fusion | flops 266240000 | bytes 2954240 | tf_op jit(solution)/shard_map/oc,cwh->owh/dot_general | solution.py:28
  24.8 0.8 %fusion.26 = f32[10,130,320]{2,1,0:T(8,128)S(1)} fusion(bf16[320,12,132]{0,2,1:T(8,128)(2,1)S(1)} %pad_maximum_fusion, bf16[9,320,320]{2,1,0:T(8,128)(2,1)S(1)} %copy-done.5), kind=kOutput, calls=%fused_computation.50 | convolution fusion | flops 266240000 | bytes 2954240 | tf_op jit(solution)/shard_map/oc,cwh->owh/dot_general | solution.py:28
  25.6 0.8 %fusion.28 = f32[10,130,320]{2,1,0:T(8,128)S(1)} fusion(bf16[320,12,132]{0,2,1:T(8,128)(2,1)S(1)} %pad_maximum_fusion, bf16[9,320,320]{2,1,0:T(8,128)(2,1)S(1)} %copy-done.5), kind=kOutput, calls=%fused_computation.52 | convolution fusion | flops 266240000 | bytes 2954240 | tf_op jit(solution)/shard_map/oc,cwh->owh/dot_general | solution.py:28
  26.4 0.8 %fusion.79 = f32[10,130,320]{2,1,0:T(8,128)S(1)} fusion(bf16[9,320,320]{2,1,0:T(8,128)(2,1)S(1)} %copy-done.5, bf16[320,2,128]{0,2,1:T(8,128)(2,1)S(1)} %collective-permute-done.1, bf16[320,8,128]{0,2,1:T(8,128)(2,1)S(1)} %copy.29, bf16[320,2,128]{0,2,1:T(8,128)(2,1)S(1)} %collective-permute-done, bf16[320,12,2]{0,2,1:T(2,128)(2,1)S(1)} %collective-permute-done.2), kind=kOutput, calls=%fused_computation.103 | convolution fusion | flops 270233600 | bytes 3107840 | tf_op jit(solution)/shard_map/oc,cwh->owh/dot_general | solution.py:28
  27.2 0.8 fusion.81
  28.0 0.8 %fusion.84 = f32[10,130,320]{2,1,0:T(8,128)S(1)} fusion(bf16[9,320,320]{2,1,0:T(8,128)(2,1)S(1)} %copy-done.5, bf16[320,2,128]{0,2,1:T(8,128)(2,1)S(1)} %collective-permute-done.1, bf16[320,8,128]{0,2,1:T(8,128)(2,1)S(1)} %copy.29, bf16[320,2,128]{0,2,1:T(8,128)(2,1)S(1)} %collective-permute-done, bf16[320,12,2]{0,2,1:T(2,128)(2,1)S(1)} %collective-permute-done.2), kind=kOutput, calls=%fused_computation.108 | convolution fusion | flops 270233600 | bytes 3107840 | tf_op jit(solution)/shard_map/oc,cwh->owh/dot_general | solution.py:28
  28.8 0.8 fusion.86
  29.7 0.8 %fusion.89 = f32[10,130,320]{2,1,0:T(8,128)S(1)} fusion(bf16[9,320,320]{2,1,0:T(8,128)(2,1)S(1)} %copy-done.5, bf16[320,2,128]{0,2,1:T(8,128)(2,1)S(1)} %collective-permute-done.1, bf16[320,8,128]{0,2,1:T(8,128)(2,1)S(1)} %copy.29, bf16[320,2,128]{0,2,1:T(8,128)(2,1)S(1)} %collective-permute-done, bf16[320,12,2]{0,2,1:T(2,128)(2,1)S(1)} %collective-permute-done.2), kind=kOutput, calls=%fused_computation.113 | convolution fusion | flops 270233600 | bytes 3107840 | tf_op jit(solution)/shard_map/oc,cwh->owh/dot_general | solution.py:28
  30.5 2.3 %fusion.5 = bf16[320,10,130]{0,2,1:T(8,128)(2,1)S(1)} fusion(f32[10,130,320]{2,1,0:T(8,128)S(1)} %fusion.24, f32[10,130,320]{2,1,0:T(8,128)S(1)} %fusion.79, f32[10,130,320]{2,1,0:T(8,128)S(1)} %fusion.81, f32[10,130,320]{2,1,0:T(8,128)S(1)} %fusion.26, f32[10,130,320]{2,1,0:T(8,128)S(1)} %fusion.84, f32[10,130,320]{2,1,0:T(8,128)S(1)} %fusion.86, ...), kind=kOutput, calls=%fused_computation.9 | convolution fusion | flops 276473600 | bytes 18993664 | tf_op jit(solution)/shard_map/oc,cwh->owh/dot_general | solution.py:28
  38.0 1.7 %fusion.122 = (bf16[320,8,128]{2,0,1:T(8,128)(2,1)}, f32[320,8,128]{2,0,1:T(8,128)S(1)}) fusion(f32[320,8,128]{2,1,0:T(8,128)S(1)} %copy-done.3, f32[320]{0:T(512)S(1)} %copy-done.9, f32[8,128,320]{1,2,0:T(8,128)S(1)} %convolution_add_fusion.2, bf16[9,320,320]{2,1,0:T(8,128)(2,1)S(1)} %copy-done.2, bf16[320,10,130]{0,2,1:T(8,128)(2,1)S(1)} %fusion.5), kind=kOutput, calls=%fused_computation.152 | convolution fusion | flops 212336640 | bytes 5621760 | tf_op jit(solution)/shard_map/oc,cwh->owh/dot_general | solution.py:28
  39.8 5.2 %all-to-all-start = ((bf16[320,8,128]{2,0,1:T(8,128)(2,1)}), bf16[320,8,128]{2,0,1:T(8,128)(2,1)}, u32[]{:S(2)}, u32[]{:S(2)}) async-start(bf16[320,8,128]{2,0,1:T(8,128)(2,1)} %get-tuple-element.12), calls=%async_computation | async-start | bytes 1310720 | tf_op jit(solution)/shard_map/all_to_all | solution.py:67
  45.0 2.1 %fusion.10 = bf16[320,4,514]{2,0,1:T(8,128)(2,1)S(1)} fusion(bf16[320,1,512]{2,0,1:T(8,128)(2,1)} %collective-permute-done.5, bf16[320,2,512]{2,0,1:T(8,128)(2,1)S(1)} %copy.64, bf16[320,1,512]{2,0,1:T(8,128)(2,1)} %collective-permute-done.4), kind=kLoop, calls=%fused_computation.14 | loop fusion | flops 7895040 | bytes 2626560 | tf_op jit(solution)/shard_map/concatenate | solution.py:16
  50.0 1.5 %convolution_bitcast_fusion.3 = f32[320,2,512]{2,0,1:T(8,128)S(1)} fusion(bf16[320,1,512]{2,0,1:T(8,128)(2,1)} %collective-permute-done.5, bf16[320,2,512]{2,0,1:T(8,128)(2,1)S(1)} %copy.64, bf16[9,320,320]{2,1,0:T(8,128)(2,1)S(1)} %copy-done.1), kind=kOutput, calls=%fused_computation.38 | convolution fusion | flops 211025920 | bytes 2539520 | tf_op jit(solution)/shard_map/oc,cwh->owh/dot_general | solution.py:28
  51.5 1.5 %fusion.50 = f32[2,512,320]{1,2,0:T(8,128)S(1)} fusion(bf16[320,2,512]{2,0,1:T(8,128)(2,1)S(1)} %copy.64, bf16[320,1,512]{2,0,1:T(8,128)(2,1)} %collective-permute-done.4, bf16[9,320,320]{2,1,0:T(8,128)(2,1)S(1)} %copy-done.1), kind=kOutput, calls=%fused_computation.76 | convolution fusion | flops 211025920 | bytes 2539520 | tf_op jit(solution)/shard_map/oc,cwh->owh/dot_general | solution.py:28
  53.0 1.9 %fusion.23 = f32[320,2,512]{2,0,1:T(8,128)} fusion(f32[320,2,512]{2,0,1:T(8,128)S(1)} %convolution_bitcast_fusion.2, f32[320,2,512]{2,0,1:T(8,128)S(1)} %convolution_bitcast_fusion.3, f32[320,2,512]{2,0,1:T(8,128)S(1)} %convolution_bitcast_fusion.4, f32[320,2,512]{2,0,1:T(8,128)S(1)} %convolution_bitcast_fusion.5, f32[320,2,512]{2,0,1:T(8,128)S(1)} %fusion.59, ...), kind=kOutput, calls=%fused_computation.42 | convolution fusion | flops 212664320 | bytes 12699648 | tf_op jit(solution)/shard_map/oc,cwh->owh/dot_general | solution.py:28
  55.3 3.7 %fusion.123 = (bf16[320,2,512]{2,0,1:T(8,128)(2,1)S(1)}, f32[320,2,512]{2,0,1:T(8,128)}) fusion(bf16[4,2,40,8,128]{4,3,2,1,0:T(8,128)(2,1)} %bitcast.72, bf16[320,320]{1,0:T(8,128)(2,1)S(1)} %copy-done, f32[320,2,512]{2,1,0:T(2,128)} %param.11, f32[320,2,512]{2,0,1:T(8,128)} %fusion.23), kind=kOutput, calls=%fused_computation.153 | convolution fusion | flops 212008960 | bytes 5447680 | tf_op jit(solution)/shard_map/oc,cwh->owh/dot_general | solution.py:35
  59.0 1.9 %copy.43 = bf16[320,2,512]{0,1,2:T(2,128)(2,1)} copy(bf16[320,2,512]{2,0,1:T(8,128)(2,1)S(1)} %get-tuple-element.14) | data formatting | bytes 1310720 | tf_op jit(solution)/shard_map/convert_element_type | solution.py:69
  60.8 4.0 %all-to-all-start.1 = ((bf16[320,2,512]{0,1,2:T(2,128)(2,1)}), bf16[320,2,512]{0,1,2:T(2,128)(2,1)S(1)}, u32[]{:S(2)}, u32[]{:S(2)}) async-start(bf16[320,2,512]{0,1,2:T(2,128)(2,1)} %copy.43), calls=%async_computation.1 | async-start | bytes 1572864 | tf_op jit(solution)/shard_map/all_to_all | solution.py:70
  64.8 3.4 %copy.46 = f32[320,2,512]{2,1,0:T(2,128)} copy(f32[320,2,512]{2,0,1:T(8,128)} %get-tuple-element.15) | data formatting | bytes 2621440
  68.3 8.2 %all-to-all-done.1 = bf16[320,2,512]{0,1,2:T(2,128)(2,1)S(1)} async-done(((bf16[320,2,512]{0,1,2:T(2,128)(2,1)}), bf16[320,2,512]{0,1,2:T(2,128)(2,1)S(1)}, u32[]{:S(2)}, u32[]{:S(2)}) %all-to-all-start.1) | async-done | bytes 655392 | tf_op jit(solution)/shard_map/all_to_all | solution.py:70
  76.4 1.2 %copy.44 = bf16[320,2,4,128]{3,0,1,2:T(8,128)(2,1)S(1)} copy(bf16[320,2,4,128]{0,1,3,2:T(2,128)(2,1)S(1)} %bitcast.184) | data formatting | bytes 1310720 | tf_op jit(solution)/shard_map/all_to_all | solution.py:70
  78.2 1.8 %copy.45 = f32[320,8,128]{2,1,0:T(8,128)} copy(f32[320,8,128]{2,0,1:T(8,128)S(1)} %fusion.20) | data formatting | bytes 2621440
  (47 shorter events, 10.4 us)
Async XLA Ops:
  0.6 54.7 %copy-start = (bf16[320,320]{1,0:T(8,128)(2,1)S(1)}, bf16[320,320]{1,0:T(8,128)(2,1)}, u32[]{:S(2)}) copy-start(bf16[320,320]{1,0:T(8,128)(2,1)} %param.18) | copy-start | bytes 614404
  0.6 9.5 %copy-start.4 = (f32[320,2,512]{2,1,0:T(2,128)S(1)}, f32[320,2,512]{2,1,0:T(2,128)}, u32[]{:S(2)}) copy-start(f32[320,2,512]{2,1,0:T(2,128)} %param.11) | copy-start | bytes 3932164
  3.3 14.5 %collective-permute-start.1 = (bf16[320,2,128]{0,2,1:T(8,128)(2,1)}, bf16[320,2,128]{0,2,1:T(8,128)(2,1)S(1)}, u32[]{:S(2)}, u32[]{:S(2)}) collective-permute-start(bf16[320,2,128]{0,2,1:T(8,128)(2,1)} %get-tuple-element.9), channel_id=1, source_target_pairs={{4,0},{8,4},{12,8},{5,1},{9,5},{13,9},{6,2},{10,6},{14,10},{7,3},{... | collective-permute-start | bytes 491528 | tf_op jit(solution)/shard_map/ppermute | solution.py:15
  4.5 13.2 %collective-permute-start = (bf16[320,2,128]{0,2,1:T(8,128)(2,1)}, bf16[320,2,128]{0,2,1:T(8,128)(2,1)S(1)}, u32[]{:S(2)}, u32[]{:S(2)}) collective-permute-start(bf16[320,2,128]{0,2,1:T(8,128)(2,1)} %get-tuple-element.8), channel_id=1, source_target_pairs={{0,4},{4,8},{8,12},{1,5},{5,9},{9,13},{2,6},{6,10},{10,14},{3,7},{... | collective-permute-start | bytes 491528 | tf_op jit(solution)/shard_map/ppermute | solution.py:14
  11.2 33.7 %collective-permute-start.5 = (bf16[320,1,512]{2,0,1:T(8,128)(2,1)}, bf16[320,1,512]{2,0,1:T(8,128)(2,1)}, u32[]{:S(2)}, u32[]{:S(2)}) collective-permute-start(bf16[320,1,512]{2,0,1:T(8,128)(2,1)} %get-tuple-element.11), channel_id=1, source_target_pairs={{1,0},{2,1},{3,2},{4,3},{5,4},{6,5},{7,6},{8,7},{9,8},{10,9},{11,1... | collective-permute-start | bytes 983048 | tf_op jit(solution)/shard_map/ppermute | solution.py:15
  12.5 32.5 %collective-permute-start.4 = (bf16[320,1,512]{2,0,1:T(8,128)(2,1)}, bf16[320,1,512]{2,0,1:T(8,128)(2,1)}, u32[]{:S(2)}, u32[]{:S(2)}) collective-permute-start(bf16[320,1,512]{2,0,1:T(8,128)(2,1)} %get-tuple-element.10), channel_id=1, source_target_pairs={{0,1},{1,2},{2,3},{3,4},{4,5},{5,6},{6,7},{7,8},{8,9},{9,10},{10,1... | collective-permute-start | bytes 983048 | tf_op jit(solution)/shard_map/ppermute | solution.py:14
  17.8 6.2 %copy-start.5 = (bf16[9,320,320]{2,1,0:T(8,128)(2,1)S(1)}, bf16[9,320,320]{2,1,0:T(8,128)(2,1)}, u32[]{:S(2)}) copy-start(bf16[9,320,320]{2,1,0:T(8,128)(2,1)} %param.12) | copy-start | bytes 5529604
  17.8 4.9 %collective-permute-start.3 = (bf16[320,12,2]{0,2,1:T(2,128)(2,1)S(1)}, bf16[320,12,2]{0,2,1:T(2,128)(2,1)S(1)}, u32[]{:S(2)}, u32[]{:S(2)}) collective-permute-start(bf16[320,12,2]{0,2,1:T(2,128)(2,1)S(1)} %get-tuple-element.7), channel_id=1, source_target_pairs={{1,0},{2,1},{3,2},{5,4},{6,5},{7,6},{9,8},{10,9},{11,10},{13,12},{... | collective-permute-start | bytes 46088 | tf_op jit(solution)/shard_map/ppermute | solution.py:15
  19.3 4.2 %collective-permute-start.2 = (bf16[320,12,2]{0,2,1:T(2,128)(2,1)S(1)}, bf16[320,12,2]{0,2,1:T(2,128)(2,1)S(1)}, u32[]{:S(2)}, u32[]{:S(2)}) collective-permute-start(bf16[320,12,2]{0,2,1:T(2,128)(2,1)S(1)} %get-tuple-element.6), channel_id=1, source_target_pairs={{0,1},{1,2},{2,3},{4,5},{5,6},{6,7},{8,9},{9,10},{10,11},{12,13},{... | collective-permute-start | bytes 46088 | tf_op jit(solution)/shard_map/ppermute | solution.py:14
  29.6 0.8 %copy-start.8 = (f32[320]{0:T(512)S(1)}, f32[320]{0:T(512)}, u32[]{:S(2)}) copy-start(f32[320]{0:T(512)} %param.15) | copy-start | bytes 3844
  30.5 2.4 %copy-start.2 = (bf16[9,320,320]{2,1,0:T(8,128)(2,1)S(1)}, bf16[9,320,320]{2,1,0:T(8,128)(2,1)}, u32[]{:S(2)}) copy-start(bf16[9,320,320]{2,1,0:T(8,128)(2,1)} %param.13) | copy-start | bytes 5529604
  36.7 1.3 %copy-start.3 = (f32[320,8,128]{2,1,0:T(8,128)S(1)}, f32[320,8,128]{2,1,0:T(8,128)}, u32[]{:S(2)}) copy-start(f32[320,8,128]{2,1,0:T(8,128)} %param.10) | copy-start | bytes 3932164
  36.7 1.3 %copy-start.9 = (f32[320]{0:T(512)S(1)}, f32[320]{0:T(512)}, u32[]{:S(2)}) copy-start(f32[320]{0:T(512)} %param.16) | copy-start | bytes 3844
  39.8 15.5 %all-to-all-start = ((bf16[320,8,128]{2,0,1:T(8,128)(2,1)}), bf16[320,8,128]{2,0,1:T(8,128)(2,1)}, u32[]{:S(2)}, u32[]{:S(2)}) async-start(bf16[320,8,128]{2,0,1:T(8,128)(2,1)} %get-tuple-element.12), calls=%async_computation | async-start | bytes 1310720 | tf_op jit(solution)/shard_map/all_to_all | solution.py:67
  45.0 2.1 %copy-start.1 = (bf16[9,320,320]{2,1,0:T(8,128)(2,1)S(1)}, bf16[9,320,320]{2,1,0:T(8,128)(2,1)}, u32[]{:S(2)}) copy-start(bf16[9,320,320]{2,1,0:T(8,128)(2,1)} %param.14) | copy-start | bytes 5529604
  51.5 1.5 %copy-start.7 = (f32[320]{0:T(512)S(1)}, f32[320]{0:T(512)}, u32[]{:S(2)}) copy-start(f32[320]{0:T(512)} %param.17) | copy-start | bytes 3844
  60.8 15.6 %all-to-all-start.1 = ((bf16[320,2,512]{0,1,2:T(2,128)(2,1)}), bf16[320,2,512]{0,1,2:T(2,128)(2,1)S(1)}, u32[]{:S(2)}, u32[]{:S(2)}) async-start(bf16[320,2,512]{0,1,2:T(2,128)(2,1)} %copy.43), calls=%async_computation.1 | async-start | bytes 1572864 | tf_op jit(solution)/shard_map/all_to_all | solution.py:70
  64.8 12.8 %copy-start.6 = (bf16[320,320]{1,0:T(8,128)(2,1)S(1)}, bf16[320,320]{1,0:T(8,128)(2,1)}, u32[]{:S(2)}) copy-start(bf16[320,320]{1,0:T(8,128)(2,1)} %param.19) | copy-start | bytes 614404
where the time goes:
time: 80.5 us; the launch traced here: 80 us
  matrix products  28.2 us (35%)
  starting transfers between devices  25.9 us (32%)
  local copies, waits for them, and re-layouts  12.8 us (16%)
  waiting for transfers between devices  9.34 us (12%)
  other arithmetic  2.73 us (3%)
  between operations  1.07 us (1%)
    dot_general x27, matrix products, convolve(): jnp.einsum('oc,cwh->owh', weight[offset], window, preferred_element_type=...  24 us
    ppermute x3, starting transfers between devices, padded_2(): before = lax.ppermute(last, axis, up)  12.7 us
    all_to_all x1, waiting for transfers between devices, per_device(): lax.all_to_all(control_send, 'rows', split_axis=2, concat_axis=1, tiled=T...  8.19 us
    unnamed x24, local copies, waits for them, and re-layouts  8.05 us
    all_to_all x1, starting transfers between devices, per_device(): lax.all_to_all(base_send, 'rows', split_axis=1, concat_axis=2, tiled=True)  5.23 us
    dot_general x2, matrix products, project(): jnp.einsum('oc,cwh->owh', matrix, field, preferred_element_type=jnp.float32)  4.17 us
    all_to_all x1, starting transfers between devices, per_device(): lax.all_to_all(control_send, 'rows', split_axis=2, concat_axis=1, tiled=T...  3.99 us
    ppermute x3, starting transfers between devices, padded_2(): after = lax.ppermute(leading, axis, down)  3.98 us
  transfers between devices with their start and end apart: 8, of which 3 were waited for; matrix products, arithmetic and copies ran while one was open for 39% of the time, Pallas kernels for 0%

commit v1 on v0

--- a/solution.py
+++ b/solution.py
@@ -67,7 +67,12 @@
     arrived = lax.all_to_all(base_send, "rows", split_axis=1, concat_axis=2, tiled=True)
     control_out = control_mid + project(to_control, arrived)
     control_send = control_out.astype(jnp.bfloat16)
-    returned = lax.all_to_all(control_send, "rows", split_axis=2, concat_axis=1, tiled=True)
+    returned = jnp.concatenate(
+        lax.all_to_all(
+            jnp.stack(jnp.split(control_send, lax.axis_size("rows"), axis=2)), "rows", 0, 0
+        ),
+        axis=1,
+    )
     base_out = base_mid + project(to_base, returned)
     return (base_out, control_out)
 

time: 80.5 us -> 77 us (0.957)
  local copies, waits for them, and re-layouts: 12.8 us -> 8.47 us
  other arithmetic: 2.73 us -> 3.65 us
    convert_element_type x1 -> x0, local copies, waits for them, and re-layouts: 1.86 us -> none  [per_device(): control_send = control_out.astype(jnp.bfloat16)]
    unnamed x24 -> x22, local copies, waits for them, and re-layouts: 8.05 us -> 6.69 us
    all_to_all x1 -> x0, local copies, waits for them, and re-layouts: 1.18 us -> none  [per_device(): lax.all_to_all(control_send, 'rows', split_axis=2, concat_axis=1, tiled=T...]
    another operation x0 -> x1, other arithmetic: none -> 0.92 us  [per_device(): jnp.stack(jnp.split(control_send, lax.axis_size('rows'), axis=2))]
where the time goes in v1:
time: 77 us; the launch traced here: 76.5 us
  matrix products  28 us (36%)
  starting transfers between devices  25.9 us (34%)
  waiting for transfers between devices  9.29 us (12%)
  local copies, waits for them, and re-layouts  8.47 us (11%)
  other arithmetic  3.65 us (5%)
  between operations  1.07 us (1%)
    dot_general x27, matrix products, convolve(): jnp.einsum('oc,cwh->owh', weight[offset], window, preferred_element_type=...  24 us
    ppermute x3, starting transfers between devices, padded_2(): before = lax.ppermute(last, axis, up)  12.7 us
    all_to_all x1, waiting for transfers between devices, per_device(): lax.all_to_all(jnp.stack(jnp.split(control_send, lax.axis_size('rows'), a...  8.15 us
    unnamed x22, local copies, waits for them, and re-layouts  6.69 us
    all_to_all x1, starting transfers between devices, per_device(): lax.all_to_all(base_send, 'rows', split_axis=1, concat_axis=2, tiled=True)  5.23 us
    dot_general x2, matrix products, project(): jnp.einsum('oc,cwh->owh', matrix, field, preferred_element_type=jnp.float32)  4.05 us
    all_to_all x1, starting transfers between devices, per_device(): lax.all_to_all(jnp.stack(jnp.split(control_send, lax.axis_size('rows'), a...  3.99 us
    ppermute x3, starting transfers between devices, padded_2(): after = lax.ppermute(leading, axis, down)  3.98 us
  transfers between devices with their start and end apart: 8, of which 3 were waited for; matrix products, arithmetic and copies ran while one was open for 39% of the time, Pallas kernels for 0%

profile of v1, /device:TPU:0, one launch (start us, length us, event | category | flops | bytes accessed | tf_op | source)
XLA Modules:
  0.0 76.5 jit_solution(6459789452707213470)
XLA Ops:
  0.7 1.8 %copy.12 = bf16[320,8,128]{0,2,1:T(8,128)(2,1)S(1)} copy(f32[320,8,128]{2,1,0:T(8,128)} %param.10) | data formatting | bytes 1966080 | tf_op args[0]
  2.5 0.8 %fusion.120 = (bf16[320,2,128]{0,2,1:T(8,128)(2,1)}, bf16[320,2,128]{0,2,1:T(8,128)(2,1)}) fusion(bf16[320,8,128]{0,2,1:T(8,128)(2,1)S(1)} %copy.12), kind=kLoop, calls=%fused_computation.155 | loop fusion | bytes 655360 | tf_op jit(solution)/shard_map/slice | solution.py:12
  3.3 1.3 %collective-permute-start.1 = (bf16[320,2,128]{0,2,1:T(8,128)(2,1)}, bf16[320,2,128]{0,2,1:T(8,128)(2,1)S(1)}, u32[]{:S(2)}, u32[]{:S(2)}) collective-permute-start(bf16[320,2,128]{0,2,1:T(8,128)(2,1)} %get-tuple-element.7), channel_id=1, source_target_pairs={{4,0},{8,4},{12,8},{5,1},{9,5},{13,9},{6,2},{10,6},{14,10},{7,3},{... | collective-permute-start | bytes 491528 | tf_op jit(solution)/shard_map/ppermute | solution.py:15
  4.5 5.6 %collective-permute-start = (bf16[320,2,128]{0,2,1:T(8,128)(2,1)}, bf16[320,2,128]{0,2,1:T(8,128)(2,1)S(1)}, u32[]{:S(2)}, u32[]{:S(2)}) collective-permute-start(bf16[320,2,128]{0,2,1:T(8,128)(2,1)} %get-tuple-element.6), channel_id=1, source_target_pairs={{0,4},{4,8},{8,12},{1,5},{5,9},{9,13},{2,6},{6,10},{10,14},{3,7},{... | collective-permute-start | bytes 491528 | tf_op jit(solution)/shard_map/ppermute | solution.py:14
  10.4 0.9 %fusion.121 = (bf16[320,1,512]{2,0,1:T(8,128)(2,1)}, bf16[320,1,512]{2,0,1:T(8,128)(2,1)}) fusion(bf16[320,2,512]{2,0,1:T(8,128)(2,1)S(1)} %copy.45), kind=kLoop, calls=%fused_computation.156 | loop fusion | bytes 1310720 | tf_op jit(solution)/shard_map/slice | solution.py:12
  11.2 1.3 %collective-permute-start.5 = (bf16[320,1,512]{2,0,1:T(8,128)(2,1)}, bf16[320,1,512]{2,0,1:T(8,128)(2,1)}, u32[]{:S(2)}, u32[]{:S(2)}) collective-permute-start(bf16[320,1,512]{2,0,1:T(8,128)(2,1)} %get-tuple-element.13), channel_id=1, source_target_pairs={{1,0},{2,1},{3,2},{4,3},{5,4},{6,5},{7,6},{8,7},{9,8},{10,9},{11,1... | collective-permute-start | bytes 983048 | tf_op jit(solution)/shard_map/ppermute | solution.py:15
  12.5 3.8 %collective-permute-start.4 = (bf16[320,1,512]{2,0,1:T(8,128)(2,1)}, bf16[320,1,512]{2,0,1:T(8,128)(2,1)}, u32[]{:S(2)}, u32[]{:S(2)}) collective-permute-start(bf16[320,1,512]{2,0,1:T(8,128)(2,1)} %get-tuple-element.12), channel_id=1, source_target_pairs={{0,1},{1,2},{2,3},{3,4},{4,5},{5,6},{6,7},{7,8},{8,9},{9,10},{10,1... | collective-permute-start | bytes 983048 | tf_op jit(solution)/shard_map/ppermute | solution.py:14
  16.3 1.4 %fusion.59 = f32[320,2,512]{2,0,1:T(8,128)S(1)} fusion(bf16[320,2,512]{2,0,1:T(8,128)(2,1)S(1)} %copy.45, bf16[9,320,320]{2,1,0:T(8,128)(2,1)} %param.14), kind=kOutput, calls=%fused_computation.86 | convolution fusion | flops 209715200 | bytes 2211840 | tf_op jit(solution)/shard_map/oc,cwh->owh/dot_general | solution.py:28
  17.8 1.4 %collective-permute-start.3 = (bf16[320,12,2]{0,2,1:T(2,128)(2,1)S(1)}, bf16[320,12,2]{0,2,1:T(2,128)(2,1)S(1)}, u32[]{:S(2)}, u32[]{:S(2)}) collective-permute-start(bf16[320,12,2]{0,2,1:T(2,128)(2,1)S(1)} %get-tuple-element.5), channel_id=1, source_target_pairs={{1,0},{2,1},{3,2},{5,4},{6,5},{7,6},{9,8},{10,9},{11,10},{13,12},{... | collective-permute-start | bytes 46088 | tf_op jit(solution)/shard_map/ppermute | solution.py:15
  19.3 3.4 %collective-permute-start.2 = (bf16[320,12,2]{0,2,1:T(2,128)(2,1)S(1)}, bf16[320,12,2]{0,2,1:T(2,128)(2,1)S(1)}, u32[]{:S(2)}, u32[]{:S(2)}) collective-permute-start(bf16[320,12,2]{0,2,1:T(2,128)(2,1)S(1)} %get-tuple-element.4), channel_id=1, source_target_pairs={{0,1},{1,2},{2,3},{4,5},{5,6},{6,7},{8,9},{9,10},{10,11},{12,13},{... | collective-permute-start | bytes 46088 | tf_op jit(solution)/shard_map/ppermute | solution.py:14
  24.0 0.8 %fusion.24 = f32[10,130,320]{2,1,0:T(8,128)S(1)} fusion(bf16[320,12,132]{0,2,1:T(8,128)(2,1)S(1)} %pad_maximum_fusion, bf16[9,320,320]{2,1,0:T(8,128)(2,1)S(1)} %copy-done.5), kind=kOutput, calls=%fused_computation.48 | convolution fusion | flops 266240000 | bytes 2954240 | tf_op jit(solution)/shard_map/oc,cwh->owh/dot_general | solution.py:28
  24.8 0.8 %fusion.26 = f32[10,130,320]{2,1,0:T(8,128)S(1)} fusion(bf16[320,12,132]{0,2,1:T(8,128)(2,1)S(1)} %pad_maximum_fusion, bf16[9,320,320]{2,1,0:T(8,128)(2,1)S(1)} %copy-done.5), kind=kOutput, calls=%fused_computation.50 | convolution fusion | flops 266240000 | bytes 2954240 | tf_op jit(solution)/shard_map/oc,cwh->owh/dot_general | solution.py:28
  25.6 0.8 %fusion.28 = f32[10,130,320]{2,1,0:T(8,128)S(1)} fusion(bf16[320,12,132]{0,2,1:T(8,128)(2,1)S(1)} %pad_maximum_fusion, bf16[9,320,320]{2,1,0:T(8,128)(2,1)S(1)} %copy-done.5), kind=kOutput, calls=%fused_computation.52 | convolution fusion | flops 266240000 | bytes 2954240 | tf_op jit(solution)/shard_map/oc,cwh->owh/dot_general | solution.py:28
  26.4 0.8 %fusion.79 = f32[10,130,320]{2,1,0:T(8,128)S(1)} fusion(bf16[9,320,320]{2,1,0:T(8,128)(2,1)S(1)} %copy-done.5, bf16[320,2,128]{0,2,1:T(8,128)(2,1)S(1)} %collective-permute-done.1, bf16[320,8,128]{0,2,1:T(8,128)(2,1)S(1)} %copy.12, bf16[320,2,128]{0,2,1:T(8,128)(2,1)S(1)} %collective-permute-done, bf16[320,12,2]{0,2,1:T(2,128)(2,1)S(1)} %collective-permute-done.2), kind=kOutput, calls=%fused_computation.104 | convolution fusion | flops 270233600 | bytes 3107840 | tf_op jit(solution)/shard_map/oc,cwh->owh/dot_general | solution.py:28
  27.2 0.8 %fusion.81 = f32[10,130,320]{2,1,0:T(8,128)S(1)} fusion(bf16[9,320,320]{2,1,0:T(8,128)(2,1)S(1)} %copy-done.5, bf16[320,12,2]{0,2,1:T(2,128)(2,1)S(1)} %collective-permute-done.3, bf16[320,2,128]{0,2,1:T(8,128)(2,1)S(1)} %collective-permute-done.1, bf16[320,8,128]{0,2,1:T(8,128)(2,1)S(1)} %copy.12, bf16[320,2,128]{0,2,1:T(8,128)(2,1)S(1)} %collective-permute-done), kind=kOutput, calls=%fused_computation.106 | convolution fusion | flops 270233600 | bytes 3107840 | tf_op jit(solution)/shard_map/oc,cwh->owh/dot_general | solution.py:28
  28.0 0.8 %fusion.84 = f32[10,130,320]{2,1,0:T(8,128)S(1)} fusion(bf16[9,320,320]{2,1,0:T(8,128)(2,1)S(1)} %copy-done.5, bf16[320,2,128]{0,2,1:T(8,128)(2,1)S(1)} %collective-permute-done.1, bf16[320,8,128]{0,2,1:T(8,128)(2,1)S(1)} %copy.12, bf16[320,2,128]{0,2,1:T(8,128)(2,1)S(1)} %collective-permute-done, bf16[320,12,2]{0,2,1:T(2,128)(2,1)S(1)} %collective-permute-done.2), kind=kOutput, calls=%fused_computation.109 | convolution fusion | flops 270233600 | bytes 3107840 | tf_op jit(solution)/shard_map/oc,cwh->owh/dot_general | solution.py:28
  28.8 0.8 %fusion.86 = f32[10,130,320]{2,1,0:T(8,128)S(1)} fusion(bf16[9,320,320]{2,1,0:T(8,128)(2,1)S(1)} %copy-done.5, bf16[320,12,2]{0,2,1:T(2,128)(2,1)S(1)} %collective-permute-done.3, bf16[320,2,128]{0,2,1:T(8,128)(2,1)S(1)} %collective-permute-done.1, bf16[320,8,128]{0,2,1:T(8,128)(2,1)S(1)} %copy.12, bf16[320,2,128]{0,2,1:T(8,128)(2,1)S(1)} %collective-permute-done), kind=kOutput, calls=%fused_computation.111 | convolution fusion | flops 270233600 | bytes 3107840 | tf_op jit(solution)/shard_map/oc,cwh->owh/dot_general | solution.py:28
  29.7 0.8 %fusion.89 = f32[10,130,320]{2,1,0:T(8,128)S(1)} fusion(bf16[9,320,320]{2,1,0:T(8,128)(2,1)S(1)} %copy-done.5, bf16[320,2,128]{0,2,1:T(8,128)(2,1)S(1)} %collective-permute-done.1, bf16[320,8,128]{0,2,1:T(8,128)(2,1)S(1)} %copy.12, bf16[320,2,128]{0,2,1:T(8,128)(2,1)S(1)} %collective-permute-done, bf16[320,12,2]{0,2,1:T(2,128)(2,1)S(1)} %collective-permute-done.2), kind=kOutput, calls=%fused_computation.114 | convolution fusion | flops 270233600 | bytes 3107840 | tf_op jit(solution)/shard_map/oc,cwh->owh/dot_general | solution.py:28
  30.5 2.3 %fusion.5 = bf16[320,10,130]{0,2,1:T(8,128)(2,1)S(1)} fusion(f32[10,130,320]{2,1,0:T(8,128)S(1)} %fusion.24, f32[10,130,320]{2,1,0:T(8,128)S(1)} %fusion.79, f32[10,130,320]{2,1,0:T(8,128)S(1)} %fusion.81, f32[10,130,320]{2,1,0:T(8,128)S(1)} %fusion.26, f32[10,130,320]{2,1,0:T(8,128)S(1)} %fusion.84, f32[10,130,320]{2,1,0:T(8,128)S(1)} %fusion.86, ...), kind=kOutput, calls=%fused_computation.9 | convolution fusion | flops 276473600 | bytes 18993664 | tf_op jit(solution)/shard_map/oc,cwh->owh/dot_general | solution.py:28
  38.0 1.7 %fusion.122 = (bf16[320,8,128]{2,0,1:T(8,128)(2,1)}, f32[320,8,128]{2,0,1:T(8,128)S(1)}) fusion(f32[320,8,128]{2,1,0:T(8,128)S(1)} %copy-done.3, f32[320]{0:T(512)S(1)} %copy-done.8, f32[8,128,320]{1,2,0:T(8,128)S(1)} %convolution_add_fusion.2, bf16[9,320,320]{2,1,0:T(8,128)(2,1)S(1)} %copy-done.2, bf16[320,10,130]{0,2,1:T(8,128)(2,1)S(1)} %fusion.5), kind=kOutput, calls=%fused_computation.157 | convolution fusion | flops 212336640 | bytes 5621760 | tf_op jit(solution)/shard_map/oc,cwh->owh/dot_general | solution.py:28
  39.8 5.2 %all-to-all-start = ((bf16[320,8,128]{2,0,1:T(8,128)(2,1)}), bf16[320,8,128]{2,0,1:T(8,128)(2,1)}, u32[]{:S(2)}, u32[]{:S(2)}) async-start(bf16[320,8,128]{2,0,1:T(8,128)(2,1)} %get-tuple-element.14), calls=%async_computation | async-start | bytes 1310720 | tf_op jit(solution)/shard_map/all_to_all | solution.py:67
  45.0 2.1 %fusion.10 = bf16[320,4,514]{2,0,1:T(8,128)(2,1)S(1)} fusion(bf16[320,1,512]{2,0,1:T(8,128)(2,1)} %collective-permute-done.5, bf16[320,2,512]{2,0,1:T(8,128)(2,1)S(1)} %copy.45, bf16[320,1,512]{2,0,1:T(8,128)(2,1)} %collective-permute-done.4), kind=kLoop, calls=%fused_computation.14 | loop fusion | flops 7895040 | bytes 2626560 | tf_op jit(solution)/shard_map/concatenate | solution.py:16
  50.0 1.5 %convolution_bitcast_fusion.3 = f32[320,2,512]{2,0,1:T(8,128)S(1)} fusion(bf16[320,1,512]{2,0,1:T(8,128)(2,1)} %collective-permute-done.5, bf16[320,2,512]{2,0,1:T(8,128)(2,1)S(1)} %copy.45, bf16[9,320,320]{2,1,0:T(8,128)(2,1)S(1)} %copy-done.1), kind=kOutput, calls=%fused_computation.38 | convolution fusion | flops 211025920 | bytes 2539520 | tf_op jit(solution)/shard_map/oc,cwh->owh/dot_general | solution.py:28
  51.5 1.5 %fusion.50 = f32[2,512,320]{1,2,0:T(8,128)S(1)} fusion(bf16[320,2,512]{2,0,1:T(8,128)(2,1)S(1)} %copy.45, bf16[320,1,512]{2,0,1:T(8,128)(2,1)} %collective-permute-done.4, bf16[9,320,320]{2,1,0:T(8,128)(2,1)S(1)} %copy-done.1), kind=kOutput, calls=%fused_computation.76 | convolution fusion | flops 211025920 | bytes 2539520 | tf_op jit(solution)/shard_map/oc,cwh->owh/dot_general | solution.py:28
  53.0 1.9 %fusion.23 = f32[320,2,512]{2,0,1:T(8,128)} fusion(f32[320,2,512]{2,0,1:T(8,128)S(1)} %convolution_bitcast_fusion.2, f32[320,2,512]{2,0,1:T(8,128)S(1)} %convolution_bitcast_fusion.3, f32[320,2,512]{2,0,1:T(8,128)S(1)} %convolution_bitcast_fusion.4, f32[320,2,512]{2,0,1:T(8,128)S(1)} %convolution_bitcast_fusion.5, f32[320,2,512]{2,0,1:T(8,128)S(1)} %fusion.59, ...), kind=kOutput, calls=%fused_computation.42 | convolution fusion | flops 212664320 | bytes 12699648 | tf_op jit(solution)/shard_map/oc,cwh->owh/dot_general | solution.py:28
  55.3 2.6 %fusion.123 = (bf16[320,2,512]{2,0,1:T(8,128)(2,1)S(1)}, f32[320,2,512]{2,0,1:T(8,128)S(1)}) fusion(bf16[4,2,40,8,128]{4,3,2,1,0:T(8,128)(2,1)} %bitcast.75, bf16[320,320]{1,0:T(8,128)(2,1)S(1)} %copy-done, f32[320,2,512]{2,1,0:T(2,128)} %param.11, f32[320,2,512]{2,0,1:T(8,128)} %fusion.23), kind=kOutput, calls=%fused_computation.158 | convolution fusion | flops 212008960 | bytes 5447680 | tf_op jit(solution)/shard_map/oc,cwh->owh/dot_general | solution.py:35
  58.0 0.9 %pad_maximum_fusion.6 = bf16[4,320,2,128]{3,1,2,0:T(8,128)(2,1)} fusion(bf16[1,320,2,128]{3,1,2,0:T(8,128)(2,1)S(1)} %get-tuple-element.9, bf16[1,320,2,128]{3,1,2,0:T(8,128)(2,1)S(1)} %get-tuple-element.10, bf16[1,320,2,128]{3,1,2,0:T(8,128)(2,1)S(1)} %get-tuple-element.11, bf16[1,320,2,128]{3,1,2,0:T(8,128)(2,1)S(1)} %get-tuple-element.8), kind=kLoop, calls=%fused_computation.79 | loop fusion | flops 983040 | bytes 1310720 | tf_op jit(solution)/shard_map/stack | solution.py:72
  59.0 4.0 %all-to-all-start.1 = ((bf16[4,320,2,128]{3,1,2,0:T(8,128)(2,1)}), bf16[4,320,2,128]{3,1,2,0:T(8,128)(2,1)S(1)}, u32[]{:S(2)}, u32[]{:S(2)}) async-start(bf16[4,320,2,128]{3,1,2,0:T(8,128)(2,1)} %pad_maximum_fusion.6), calls=%async_computation.1 | async-start | bytes 1310720 | tf_op jit(solution)/shard_map/all_to_all | solution.py:71
  63.0 2.1 %copy.27 = f32[320,2,512]{2,1,0:T(2,128)} copy(f32[320,2,512]{2,0,1:T(8,128)S(1)} %get-tuple-element.17) | data formatting | bytes 2621440
  65.0 8.2 %all-to-all-done.1 = bf16[4,320,2,128]{3,1,2,0:T(8,128)(2,1)S(1)} async-done(((bf16[4,320,2,128]{3,1,2,0:T(8,128)(2,1)}), bf16[4,320,2,128]{3,1,2,0:T(8,128)(2,1)S(1)}, u32[]{:S(2)}, u32[]{:S(2)}) %all-to-all-start.1) | async-done | bytes 655392 | tf_op jit(solution)/shard_map/all_to_all | solution.py:71
  73.2 1.4 %fusion.20 = f32[320,8,128]{2,0,1:T(8,128)S(1)} fusion(f32[320,8,128]{2,0,1:T(8,128)S(1)} %get-tuple-element.15, bf16[320,8,128]{2,0,1:T(8,128)(2,1)S(1)} %bitcast.191, bf16[320,320]{1,0:T(8,128)(2,1)} %param.19), kind=kOutput, calls=%fused_computation.34 | convolution fusion | flops 210042880 | bytes 3481600 | tf_op jit(solution)/shard_map/oc,cwh->owh/dot_general | solution.py:35
  74.6 1.8 %copy.26 = f32[320,8,128]{2,1,0:T(8,128)} copy(f32[320,8,128]{2,0,1:T(8,128)S(1)} %fusion.20) | data formatting | bytes 2621440
  (45 shorter events, 10.0 us)
Async XLA Ops:
  0.6 54.7 %copy-start = (bf16[320,320]{1,0:T(8,128)(2,1)S(1)}, bf16[320,320]{1,0:T(8,128)(2,1)}, u32[]{:S(2)}) copy-start(bf16[320,320]{1,0:T(8,128)(2,1)} %param.18) | copy-start | bytes 614404
  0.6 9.5 %copy-start.4 = (f32[320,2,512]{2,1,0:T(2,128)S(1)}, f32[320,2,512]{2,1,0:T(2,128)}, u32[]{:S(2)}) copy-start(f32[320,2,512]{2,1,0:T(2,128)} %param.11) | copy-start | bytes 3932164
  3.3 14.5 %collective-permute-start.1 = (bf16[320,2,128]{0,2,1:T(8,128)(2,1)}, bf16[320,2,128]{0,2,1:T(8,128)(2,1)S(1)}, u32[]{:S(2)}, u32[]{:S(2)}) collective-permute-start(bf16[320,2,128]{0,2,1:T(8,128)(2,1)} %get-tuple-element.7), channel_id=1, source_target_pairs={{4,0},{8,4},{12,8},{5,1},{9,5},{13,9},{6,2},{10,6},{14,10},{7,3},{... | collective-permute-start | bytes 491528 | tf_op jit(solution)/shard_map/ppermute | solution.py:15
  4.5 13.2 %collective-permute-start = (bf16[320,2,128]{0,2,1:T(8,128)(2,1)}, bf16[320,2,128]{0,2,1:T(8,128)(2,1)S(1)}, u32[]{:S(2)}, u32[]{:S(2)}) collective-permute-start(bf16[320,2,128]{0,2,1:T(8,128)(2,1)} %get-tuple-element.6), channel_id=1, source_target_pairs={{0,4},{4,8},{8,12},{1,5},{5,9},{9,13},{2,6},{6,10},{10,14},{3,7},{... | collective-permute-start | bytes 491528 | tf_op jit(solution)/shard_map/ppermute | solution.py:14
  11.2 33.7 %collective-permute-start.5 = (bf16[320,1,512]{2,0,1:T(8,128)(2,1)}, bf16[320,1,512]{2,0,1:T(8,128)(2,1)}, u32[]{:S(2)}, u32[]{:S(2)}) collective-permute-start(bf16[320,1,512]{2,0,1:T(8,128)(2,1)} %get-tuple-element.13), channel_id=1, source_target_pairs={{1,0},{2,1},{3,2},{4,3},{5,4},{6,5},{7,6},{8,7},{9,8},{10,9},{11,1... | collective-permute-start | bytes 983048 | tf_op jit(solution)/shard_map/ppermute | solution.py:15
  12.5 32.5 %collective-permute-start.4 = (bf16[320,1,512]{2,0,1:T(8,128)(2,1)}, bf16[320,1,512]{2,0,1:T(8,128)(2,1)}, u32[]{:S(2)}, u32[]{:S(2)}) collective-permute-start(bf16[320,1,512]{2,0,1:T(8,128)(2,1)} %get-tuple-element.12), channel_id=1, source_target_pairs={{0,1},{1,2},{2,3},{3,4},{4,5},{5,6},{6,7},{7,8},{8,9},{9,10},{10,1... | collective-permute-start | bytes 983048 | tf_op jit(solution)/shard_map/ppermute | solution.py:14
  17.8 6.2 %copy-start.5 = (bf16[9,320,320]{2,1,0:T(8,128)(2,1)S(1)}, bf16[9,320,320]{2,1,0:T(8,128)(2,1)}, u32[]{:S(2)}) copy-start(bf16[9,320,320]{2,1,0:T(8,128)(2,1)} %param.12) | copy-start | bytes 5529604
  17.8 4.9 %collective-permute-start.3 = (bf16[320,12,2]{0,2,1:T(2,128)(2,1)S(1)}, bf16[320,12,2]{0,2,1:T(2,128)(2,1)S(1)}, u32[]{:S(2)}, u32[]{:S(2)}) collective-permute-start(bf16[320,12,2]{0,2,1:T(2,128)(2,1)S(1)} %get-tuple-element.5), channel_id=1, source_target_pairs={{1,0},{2,1},{3,2},{5,4},{6,5},{7,6},{9,8},{10,9},{11,10},{13,12},{... | collective-permute-start | bytes 46088 | tf_op jit(solution)/shard_map/ppermute | solution.py:15
  19.3 4.2 %collective-permute-start.2 = (bf16[320,12,2]{0,2,1:T(2,128)(2,1)S(1)}, bf16[320,12,2]{0,2,1:T(2,128)(2,1)S(1)}, u32[]{:S(2)}, u32[]{:S(2)}) collective-permute-start(bf16[320,12,2]{0,2,1:T(2,128)(2,1)S(1)} %get-tuple-element.4), channel_id=1, source_target_pairs={{0,1},{1,2},{2,3},{4,5},{5,6},{6,7},{8,9},{9,10},{10,11},{12,13},{... | collective-permute-start | bytes 46088 | tf_op jit(solution)/shard_map/ppermute | solution.py:14
  29.6 0.8 %copy-start.7 = (f32[320]{0:T(512)S(1)}, f32[320]{0:T(512)}, u32[]{:S(2)}) copy-start(f32[320]{0:T(512)} %param.15) | copy-start | bytes 3844
  30.5 2.4 %copy-start.2 = (bf16[9,320,320]{2,1,0:T(8,128)(2,1)S(1)}, bf16[9,320,320]{2,1,0:T(8,128)(2,1)}, u32[]{:S(2)}) copy-start(bf16[9,320,320]{2,1,0:T(8,128)(2,1)} %param.13) | copy-start | bytes 5529604
  36.7 1.3 %copy-start.3 = (f32[320,8,128]{2,1,0:T(8,128)S(1)}, f32[320,8,128]{2,1,0:T(8,128)}, u32[]{:S(2)}) copy-start(f32[320,8,128]{2,1,0:T(8,128)} %param.10) | copy-start | bytes 3932164
  36.7 1.3 %copy-start.8 = (f32[320]{0:T(512)S(1)}, f32[320]{0:T(512)}, u32[]{:S(2)}) copy-start(f32[320]{0:T(512)} %param.16) | copy-start | bytes 3844
  39.8 15.5 %all-to-all-start = ((bf16[320,8,128]{2,0,1:T(8,128)(2,1)}), bf16[320,8,128]{2,0,1:T(8,128)(2,1)}, u32[]{:S(2)}, u32[]{:S(2)}) async-start(bf16[320,8,128]{2,0,1:T(8,128)(2,1)} %get-tuple-element.14), calls=%async_computation | async-start | bytes 1310720 | tf_op jit(solution)/shard_map/all_to_all | solution.py:67
  45.0 2.1 %copy-start.1 = (bf16[9,320,320]{2,1,0:T(8,128)(2,1)S(1)}, bf16[9,320,320]{2,1,0:T(8,128)(2,1)}, u32[]{:S(2)}) copy-start(bf16[9,320,320]{2,1,0:T(8,128)(2,1)} %param.14) | copy-start | bytes 5529604
  51.5 1.5 %copy-start.6 = (f32[320]{0:T(512)S(1)}, f32[320]{0:T(512)}, u32[]{:S(2)}) copy-start(f32[320]{0:T(512)} %param.17) | copy-start | bytes 3844
  59.0 14.2 %all-to-all-start.1 = ((bf16[4,320,2,128]{3,1,2,0:T(8,128)(2,1)}), bf16[4,320,2,128]{3,1,2,0:T(8,128)(2,1)S(1)}, u32[]{:S(2)}, u32[]{:S(2)}) async-start(bf16[4,320,2,128]{3,1,2,0:T(8,128)(2,1)} %pad_maximum_fusion.6), calls=%async_computation.1 | async-start | bytes 1310720 | tf_op jit(solution)/shard_map/all_to_all | solution.py:71
